TPU v7x, 32 devices: a whole 2x2x4 slice. The times are simulated.
32 devices in a mesh: groups: 2 (over y), seq: 8 (over z, x), tp: 2 (over core).
Axes of the slice: x: 2, y: 2, z: 4, core: 2. Of those that a mesh axis runs over, the one named last changes fastest.
Arguments:
- span_queries: bfloat16 [128, 64, 128], P(('groups', 'seq'), 'tp'), parts along dimension 0, may hold values from -180 to 180
- span_keys: bfloat16 [128, 4, 128], P(('groups', 'seq'), 'tp'), parts along dimension 0, may hold values from -9 to 9
- span_values: bfloat16 [128, 4, 128], P(('groups', 'seq'), 'tp'), parts along dimension 0, may hold values from -6.5 to 6.5
- prefix_keys: bfloat16 [1152, 4, 128], P(('groups', 'seq'), 'tp'), parts along dimension 0, may hold values from -9 to 9
- prefix_values: bfloat16 [1152, 4, 128], P(('groups', 'seq'), 'tp'), parts along dimension 0, may hold values from -6.5 to 6.5
- prefix_lengths: int32 [16], P('groups'), parts along dimension 0, may hold values from 1 to 72
- decode_queries: bfloat16 [32, 64, 128], P(('groups', 'seq'), 'tp'), parts along dimension 0, may hold values from -180 to 180
- decode_new_keys: bfloat16 [32, 4, 128], P(('groups', 'seq'), 'tp'), parts along dimension 0, may hold values from -6 to 6
- decode_new_values: bfloat16 [32, 4, 128], P(('groups', 'seq'), 'tp'), parts along dimension 0, may hold values from -6 to 6
- decode_key_cache: bfloat16 [64, 256, 4, 128], P(('groups', 'seq'), None, 'tp'), parts along dimension 0, may hold values from -6 to 6
- decode_value_cache: bfloat16 [64, 256, 4, 128], P(('groups', 'seq'), None, 'tp'), parts along dimension 0, may hold values from -6 to 6
- owner_map: int32 [32, 1], P('groups'), parts along dimension 0, may hold values from 0 to 7; in each aligned block of 16 rows (0 to 15, 16 to 31, ...) at most 4 rows name the same one
- decode_lengths: int32 [32], P('groups'), parts along dimension 0, may hold values from 1 to 256
Outputs:
- prefill_out: bfloat16 [128, 64, 128], P(('groups', 'seq'), 'tp'), parts along dimension 0
- decode_out: bfloat16 [64, 64, 128], P(('groups', 'seq'), 'tp'), parts along dimension 0
There are 2 independent parts, one for each index of `groups`. A program takes and returns all parts, laid end to end along the dimension named above; each array names one. Nothing has to cross between parts.
Inputs may be any that keep to these rules, and one draw needn't show every extreme that they name: `owner_map`: no shard owns more than 4 requests, and some shard owns exactly 4.
All inputs are finite; a program needn't handle non-finite values.
Results may differ from a plain program's by a relative error of at most 0.005.
Values may be sent and summed in bfloat16 or wider, within the bound.
No kernel may reach another device: no remote copies, remote signals or barrier semaphores. Data moves between devices by JAX's collectives and lax.ppermute only.
A program may use at most 64 MiB of HBM per device.

v0:
```python
import jax
import jax.numpy as jnp
from jax import lax
from jax.sharding import PartitionSpec as P

LOWEST = -1e30


def lookup_small(table, wanted):
    columns = jnp.arange(table.shape[0], dtype=jnp.int32)
    return jnp.sum(jnp.where(wanted[:, None] == columns[None, :], table[None, :], 0), axis=1)


def block_split(length):
    blocks = 1
    while length // blocks > 512 or length % blocks != 0:
        blocks += 1
    return blocks


def online_step(carried, queries, key_rows, value_rows, allowed):
    running_max, normalizer, weighted = carried
    scale = queries.shape[-1] ** (-0.5)
    scores = (
        jnp.einsum("tkgd,nkd->tkgn", queries, key_rows, preferred_element_type=jnp.float32) * scale
    )
    visible = allowed[:, None, None, :]
    scores = jnp.where(visible, scores, LOWEST)
    new_max = jnp.maximum(running_max, jnp.max(scores, axis=-1))
    weights = jnp.where(visible, jnp.exp(scores - new_max[..., None]), 0.0)
    factor = jnp.exp(running_max - new_max)
    normalizer = normalizer * factor + jnp.sum(weights, axis=-1)
    weighted = weighted * factor[..., None] + jnp.einsum(
        "tkgn,nkd->tkgd",
        weights.astype(jnp.bfloat16),
        value_rows,
        preferred_element_type=jnp.float32,
    )
    return (new_max, normalizer, weighted)


def guarded_step(carried, queries, key_rows, value_rows, allowed):
    return lax.cond(
        jnp.any(allowed),
        lambda inner: online_step(inner, queries, key_rows, value_rows, allowed),
        lambda inner: inner,
        carried,
    )


def fold_rows(carried, queries, key_rows, value_rows, allowed):
    length = key_rows.shape[0]
    blocks = block_split(length)
    if blocks == 1:
        return guarded_step(carried, queries, key_rows, value_rows, allowed)
    width = length // blocks
    stacked = (
        key_rows.reshape((blocks, width) + key_rows.shape[1:]),
        value_rows.reshape((blocks, width) + value_rows.shape[1:]),
        allowed.reshape(allowed.shape[0], blocks, width).transpose(1, 0, 2),
    )

    def visit(inner_carry, parts):
        return (guarded_step(inner_carry, queries, parts[0], parts[1], parts[2]), None)

    carried, unused = lax.scan(visit, carried, stacked)
    return carried


def on_device(
    span_queries,
    span_keys,
    span_values,
    prefix_keys,
    prefix_values,
    prefix_lengths,
    decode_queries,
    decode_new_keys,
    decode_new_values,
    decode_key_cache,
    decode_value_cache,
    owner_map,
    decode_lengths,
):
    device = lax.axis_index("seq")
    tokens_here, heads_here, head_dim = span_queries.shape
    kv_here = span_keys.shape[1]
    group_size = heads_here // kv_here
    queries = span_queries.reshape(tokens_here, kv_here, group_size, head_dim)
    token_index = device * tokens_here + jnp.arange(tokens_here, dtype=jnp.int32)
    prefix_here = prefix_keys.shape[0]
    initial = (
        jnp.full((tokens_here, kv_here, group_size), LOWEST, jnp.float32),
        jnp.zeros((tokens_here, kv_here, group_size), jnp.float32),
        jnp.zeros((tokens_here, kv_here, group_size, head_dim), jnp.float32),
    )
    stride = prefix_here + tokens_here
    both_keys = jnp.concatenate([prefix_keys, span_keys], axis=0)
    both_values = jnp.concatenate([prefix_values, span_values], axis=0)
    carried = initial
    key_rows = lax.all_gather(both_keys, "seq", axis=0, tiled=True)
    value_rows = lax.all_gather(both_values, "seq", axis=0, tiled=True)
    length = key_rows.shape[0]
    shards = length // stride
    tail = key_rows.shape[1:]
    keys_split = key_rows.reshape((shards, stride) + tail)
    values_split = value_rows.reshape((shards, stride) + tail)
    prefix_k = keys_split[:, :prefix_here].reshape((shards * prefix_here,) + tail)
    prefix_v = values_split[:, :prefix_here].reshape((shards * prefix_here,) + tail)
    span_k = keys_split[:, prefix_here:].reshape((shards * tokens_here,) + tail)
    span_v = values_split[:, prefix_here:].reshape((shards * tokens_here,) + tail)
    prefix_position = jnp.arange(shards * prefix_here, dtype=jnp.int32)
    prefix_ok = prefix_position % prefix_here < lookup_small(
        prefix_lengths, prefix_position // prefix_here
    )
    carried = fold_rows(
        carried,
        queries,
        prefix_k,
        prefix_v,
        jnp.broadcast_to(prefix_ok[None, :], (tokens_here, prefix_k.shape[0])),
    )
    span_position = jnp.arange(shards * tokens_here, dtype=jnp.int32)
    carried = fold_rows(
        carried, queries, span_k, span_v, span_position[None, :] <= token_index[:, None]
    )
    running_max, normalizer, weighted = carried
    prefill_out = (
        (weighted / normalizer[..., None])
        .reshape(tokens_here, heads_here, head_dim)
        .astype(jnp.bfloat16)
    )
    owners = owner_map[:, 0]
    requests = owners.shape[0]
    order = jnp.arange(requests, dtype=jnp.int32)
    earlier = (owners[None, :] == owners[:, None]) & (order[None, :] < order[:, None])
    ranking = jnp.sum(earlier.astype(jnp.int32), axis=1)
    slots_here = decode_key_cache.shape[0]
    slot_ids = jnp.arange(slots_here, dtype=jnp.int32)
    query_rows = lax.all_gather(decode_queries, "seq", axis=0, tiled=True)
    new_keys = lax.all_gather(decode_new_keys, "seq", axis=0, tiled=True)
    new_values = lax.all_gather(decode_new_values, "seq", axis=0, tiled=True)
    chosen = (owners == device)[None, :] & (ranking[None, :] == slot_ids[:, None])
    selector = chosen.astype(jnp.bfloat16)
    picked_queries = jnp.einsum(
        "sn,nhd->shd", selector, query_rows, preferred_element_type=jnp.float32
    )
    picked_keys = jnp.einsum("sn,nkd->skd", selector, new_keys, preferred_element_type=jnp.float32)
    picked_values = jnp.einsum(
        "sn,nkd->skd", selector, new_values, preferred_element_type=jnp.float32
    )
    picked_lengths = jnp.sum(jnp.where(chosen, decode_lengths[None, :], 0), axis=1)
    context = decode_key_cache.shape[1]
    grouped = picked_queries.astype(jnp.bfloat16).reshape(slots_here, kv_here, group_size, head_dim)
    own_keys = picked_keys.astype(jnp.bfloat16)
    own_values = picked_values.astype(jnp.bfloat16)
    scale = head_dim ** (-0.5)
    scores = (
        jnp.einsum("skgd,sckd->skgc", grouped, decode_key_cache, preferred_element_type=jnp.float32)
        * scale
    )
    visible = (jnp.arange(context, dtype=jnp.int32)[None, :] < picked_lengths[:, None])[
        :, None, None, :
    ]
    scores = jnp.where(visible, scores, LOWEST)
    own_score = (
        jnp.einsum("skgd,skd->skg", grouped, own_keys, preferred_element_type=jnp.float32) * scale
    )
    top_score = jnp.maximum(jnp.max(scores, axis=-1), own_score)
    weights = jnp.where(visible, jnp.exp(scores - top_score[..., None]), 0.0)
    own_weight = jnp.exp(own_score - top_score)
    total_weight = jnp.sum(weights, axis=-1) + own_weight
    rounded_own = lax.optimization_barrier(own_weight.astype(jnp.bfloat16)).astype(jnp.float32)
    mixed = jnp.einsum(
        "skgc,sckd->skgd",
        weights.astype(jnp.bfloat16),
        decode_value_cache,
        preferred_element_type=jnp.float32,
    )
    mixed = mixed + rounded_own[..., None] * own_values.astype(jnp.float32)[:, :, None, :]
    count_here = jnp.sum((owners == device).astype(jnp.int32))
    used = (slot_ids < count_here)[:, None, None, None]
    decode_out = (
        jnp.where(used, mixed / total_weight[..., None], 0.0)
        .reshape(slots_here, heads_here, head_dim)
        .astype(jnp.bfloat16)
    )
    return (prefill_out, decode_out)


def solution(mesh):
    return jax.shard_map(
        on_device,
        mesh=mesh,
        in_specs=(
            P(("groups", "seq"), "tp", None),
            P(("groups", "seq"), "tp", None),
            P(("groups", "seq"), "tp", None),
            P(("groups", "seq"), "tp", None),
            P(("groups", "seq"), "tp", None),
            P("groups"),
            P(("groups", "seq"), "tp", None),
            P(("groups", "seq"), "tp", None),
            P(("groups", "seq"), "tp", None),
            P(("groups", "seq"), None, "tp", None),
            P(("groups", "seq"), None, "tp", None),
            P("groups", None),
            P("groups"),
        ),
        out_specs=(P(("groups", "seq"), "tp", None), P(("groups", "seq"), "tp", None)),
        check_vma=False,
    )
```

profile of v0, /device:TPU:0, one launch (start us, length us, event | category | flops | bytes accessed | tf_op | source)
XLA Modules:
  0.0 148.8 jit_solution(11207647977653412298)
XLA Ops:
  0.6 0.0 copy-start
  0.6 0.0 copy-start.2
  0.7 0.7 iota_compare_fusion.3
  2.0 0.7 select_reduce_fusion
  2.8 0.1 reduce_sum.68
  2.9 0.0 copy-start.5
  2.9 0.0 copy-done.2
  2.9 0.7 copy-done.5
  3.6 0.1 pad_maximum_fusion
  3.6 32.7 %all_gather.15 = bf16[640,2,128]{2,1,0:T(2,128)(2,1)S(1)} all-gather(bf16[80,2,128]{2,1,0:T(2,128)(2,1)S(1)} %pad_maximum_fusion), channel_id=1, replica_groups=mesh['groups'=2,'seq'=8,'tp'=2] {'seq'}, dimensions={0}, use_global_device_ids=true | all-gather | bytes 368640 | tf_op jit(solution)/shard_map/all_gather | solution.py:101
  36.4 0.0 copy-start.1
  36.4 0.8 copy-done.1
  37.2 0.0 copy-start.3
  37.2 0.0 copy-start.6
  37.2 0.8 copy-done.3
  38.0 0.0 copy-done.6
  38.0 0.1 pad_maximum_fusion.1
  38.1 30.9 %all_gather.16 = bf16[640,2,128]{2,1,0:T(2,128)(2,1)S(1)} all-gather(bf16[80,2,128]{2,1,0:T(2,128)(2,1)S(1)} %pad_maximum_fusion.1), channel_id=1, replica_groups=mesh['groups'=2,'seq'=8,'tp'=2] {'seq'}, dimensions={0}, use_global_device_ids=true | all-gather | bytes 368640 | tf_op jit(solution)/shard_map/all_gather | solution.py:102
  69.1 4.4 %while.14 = (s32[]{:T(128)}, f32[8,2,16]{2,0,1:T(8,128)S(1)}, f32[8,2,16]{2,0,1:T(8,128)S(1)}, f32[8,2,16,128]{3,2,0,1:T(8,128)S(1)}, pred[2,8,288]{2,1,0:T(8,12...) while((s32[]{:T(128)}, f32[8,2,16]{2,0,1:T(8,128)S(1)}, ...), condition=%wide.region_8.9_spmd, body=%wide.region_2.8_spmd.sunk | while | flops 38480640 | bytes 1649647 | solution.py:66
  69.2 0.7 fusion.72
  70.5 0.9 conditional.4
  70.5 0.3 fusion.67
  70.8 0.2 fusion.4
  71.1 0.3 fusion.2
  71.4 0.7 fusion.72
  72.7 0.9 conditional.4
  72.7 0.3 fusion.67
  73.0 0.2 fusion.4
  73.3 0.3 fusion.2
  73.6 0.7 conditional.2
  73.6 0.3 fusion.68
  73.9 0.2 fusion.20
  74.1 0.2 fusion.16
  74.3 0.1 divide_convert_fusion
  74.5 0.0 copy-start.4
  74.5 0.6 copy.71
  75.1 0.1 copy-done.4
  75.2 30.5 %all_gather.17 = bf16[16,32,128]{2,1,0:T(8,128)(2,1)S(1)} all-gather(bf16[2,32,128]{2,1,0:T(8,128)(2,1)S(1)} %copy-done.4), channel_id=1, replica_groups=mesh['groups'=2,'seq'=8,'tp'=2] {'seq'}, dimensions={0}, use_global_device_ids=true | all-gather | bytes 147456 | tf_op jit(solution)/shard_map/all_gather | solution.py:140
  105.7 0.0 copy-start.10
  105.7 0.7 copy-done.10
  106.3 0.2 convert_reduce_fusion
  106.5 0.6 convert_reduce_fusion.1
  107.2 0.0 copy-start.9
  107.2 0.7 copy-done.9
  107.8 0.1 select_reduce_fusion.1
  107.9 0.2 convolution_convert_fusion
  108.1 0.0 copy-start.11
  108.1 0.1 iota_compare_fusion.2
  108.2 0.0 copy-done
  108.2 0.3 fusion.69
  108.5 0.0 copy-start.7
  108.5 0.7 copy-done.7
  109.2 20.5 %all_gather.18 = bf16[16,2,128]{2,1,0:T(2,128)(2,1)S(1)} all-gather(bf16[2,2,128]{2,1,0:T(2,128)(2,1)S(1)} %copy-done.7), channel_id=1, replica_groups=mesh['groups'=2,'seq'=8,'tp'=2] {'seq'}, dimensions={0}, use_global_device_ids=true | all-gather | bytes 9216 | tf_op jit(solution)/shard_map/all_gather | solution.py:141
  129.7 0.1 fusion.36
  129.8 0.1 fusion.46
  129.9 0.2 fusion.40
  130.1 0.0 copy-start.8
  130.2 0.7 copy-done.8
  130.8 16.3 %all_gather.19 = bf16[16,2,128]{2,1,0:T(2,128)(2,1)S(1)} all-gather(bf16[2,2,128]{2,1,0:T(2,128)(2,1)S(1)} %copy-done.8), channel_id=1, replica_groups=mesh['groups'=2,'seq'=8,'tp'=2] {'seq'}, dimensions={0}, use_global_device_ids=true | all-gather | bytes 9216 | tf_op jit(solution)/shard_map/all_gather | solution.py:142
  147.1 0.1 fusion.35
  147.2 0.6 iota_compare_fusion.5
  147.9 0.0 copy-done.11
  147.9 0.9 fusion.34
  (26 shorter events, 0.3 us)
Async XLA Ops:
  0.6 107.6 %copy-start = (bf16[4,256,2,128]{3,2,1,0:T(2,128)(2,1)S(1)}, bf16[4,256,2,128]{3,2,1,0:T(2,128)(2,1)}, u32[]{:S(2)}) copy-start(bf16[4,256,2,128]{3,2,1,0:T(2,128)(2,1)} %param.28) | copy-start | bytes 1572868
  0.6 2.3 %copy-start.2 = (bf16[72,2,128]{2,1,0:T(2,128)(2,1)S(1)}, bf16[72,2,128]{2,1,0:T(2,128)(2,1)}, u32[]{:S(2)}) copy-start(bf16[72,2,128]{2,1,0:T(2,128)(2,1)} %param.22) | copy-start | bytes 110596
  2.9 0.7 copy-start.5
  36.4 0.8 copy-start.1
  37.2 0.8 copy-start.3
  37.2 0.8 copy-start.6
  74.5 0.7 copy-start.4
  105.7 0.7 copy-start.10
  107.2 0.7 copy-start.9
  108.1 39.8 %copy-start.11 = (bf16[4,256,2,128]{3,2,1,0:T(2,128)(2,1)S(1)}, bf16[4,256,2,128]{3,2,1,0:T(2,128)(2,1)}, u32[]{:S(2)}) copy-start(bf16[4,256,2,128]{3,2,1,0:T(2,128)(2,1)} %param.29) | copy-start | bytes 1572868
  108.5 0.7 copy-start.7
  130.1 0.7 copy-start.8
where the time goes:
time: 149 us
  blocking collectives  131 us (88%)
  local copies, waits for them, and re-layouts  5.93 us (4%)
  other arithmetic  5.57 us (4%)
  matrix products  3.39 us (2%)
  between operations  1.53 us (1%)
  loops' own time  1.5 us (1%)
    all_gather x1, blocking collectives, on_device(): key_rows = lax.all_gather(both_keys, 'seq', axis=0, tiled=True)  32.7 us
    all_gather x1, blocking collectives, on_device(): value_rows = lax.all_gather(both_values, 'seq', axis=0, tiled=True)  30.9 us
    all_gather x1, blocking collectives, on_device(): query_rows = lax.all_gather(decode_queries, 'seq', axis=0, tiled=True)  30.5 us
    all_gather x1, blocking collectives, on_device(): new_keys = lax.all_gather(decode_new_keys, 'seq', axis=0, tiled=True)  20.5 us
    all_gather x1, blocking collectives, on_device(): new_values = lax.all_gather(decode_new_values, 'seq', axis=0, tiled=True)  16.3 us
    unnamed x24, local copies, waits for them, and re-layouts  4.99 us

commit v1 on v0

--- a/solution.py
+++ b/solution.py
@@ -137,14 +137,41 @@
     ranking = jnp.sum(earlier.astype(jnp.int32), axis=1)
     slots_here = decode_key_cache.shape[0]
     slot_ids = jnp.arange(slots_here, dtype=jnp.int32)
-    query_rows = lax.all_gather(decode_queries, "seq", axis=0, tiled=True)
     new_keys = lax.all_gather(decode_new_keys, "seq", axis=0, tiled=True)
     new_values = lax.all_gather(decode_new_values, "seq", axis=0, tiled=True)
     chosen = (owners == device)[None, :] & (ranking[None, :] == slot_ids[:, None])
     selector = chosen.astype(jnp.bfloat16)
+    length_2, index, rows = (lax.axis_size("seq"), lax.axis_index("seq"), decode_queries.shape[0])
+    forward = [(i, (i + 1) % length_2) for i in range(length_2)]
+    left = [(i, (i - 1) % length_2) for i in range(length_2)]
+    halfway = length_2 // 2
+    from_left = from_right = decode_queries
     picked_queries = jnp.einsum(
-        "sn,nhd->shd", selector, query_rows, preferred_element_type=jnp.float32
-    )
+        "sn,nhd->shd",
+        lax.dynamic_slice_in_dim(selector, index * rows, decode_queries.shape[0], axis=1),
+        decode_queries,
+        preferred_element_type=jnp.float32,
+    )
+    for step in range(1, halfway + 1):
+        from_left = lax.ppermute(from_left, "seq", forward)
+        if step < length_2 - halfway:
+            from_right = lax.ppermute(from_right, "seq", left)
+            picked_queries = picked_queries + jnp.einsum(
+                "sn,nhd->shd",
+                lax.dynamic_slice_in_dim(
+                    selector, (index + step) % length_2 * rows, from_right.shape[0], axis=1
+                ),
+                from_right,
+                preferred_element_type=jnp.float32,
+            )
+        picked_queries = picked_queries + jnp.einsum(
+            "sn,nhd->shd",
+            lax.dynamic_slice_in_dim(
+                selector, (index - step) % length_2 * rows, from_left.shape[0], axis=1
+            ),
+            from_left,
+            preferred_element_type=jnp.float32,
+        )
     picked_keys = jnp.einsum("sn,nkd->skd", selector, new_keys, preferred_element_type=jnp.float32)
     picked_values = jnp.einsum(
         "sn,nkd->skd", selector, new_values, preferred_element_type=jnp.float32

time: 149 us -> 141 us (0.946)
  blocking collectives: 131 us -> 96.3 us
  starting transfers between devices: 0 us -> 15.6 us
  waiting for transfers between devices: 0 us -> 8.49 us
  matrix products: 3.39 us -> 5.24 us
    all_gather x1 -> x0, blocking collectives: 30.5 us -> none  [on_device(): query_rows = lax.all_gather(decode_queries, 'seq', axis=0, tiled=True)]
    ppermute x0 -> x7, starting transfers between devices: none -> 15.6 us  [the longest x3 10.6 us: on_device(): from_right = lax.ppermute(from_right, 'seq', left)]
    ppermute x0 -> x7, waiting for transfers between devices: none -> 8.49 us  [the longest x4 8.48 us: on_device(): from_left = lax.ppermute(from_left, 'seq', forward)]
    all_gather x1, blocking collectives: 20.5 us -> 18.2 us  [on_device(): new_keys = lax.all_gather(decode_new_keys, 'seq', axis=0, tiled=True)]
    all_gather x1, blocking collectives: 32.7 us -> 30.9 us  [on_device(): key_rows = lax.all_gather(both_keys, 'seq', axis=0, tiled=True)]
    dot_general x1 -> x8, matrix products: 0.16 us -> 1.73 us  [the longest x4 0.86 us: on_device(): jnp.einsum('sn,nhd->shd', lax.dynamic_slice_in_dim(selector, (index - ste...]
    unnamed x24 -> x27, local copies, waits for them, and re-layouts: 4.99 us -> 5.89 us
  transfers between devices with their start and end apart: 0 -> 7, of which waited for: 0 -> 3; matrix products, arithmetic and copies ran while one was open for 0% -> 7% of each run, Pallas kernels for 0% -> 0%
where the time goes in v1:
time: 141 us
  blocking collectives  96.3 us (68%)
  starting transfers between devices  15.6 us (11%)
  waiting for transfers between devices  8.49 us (6%)
  local copies, waits for them, and re-layouts  6.82 us (5%)
  matrix products  5.24 us (4%)
  other arithmetic  5.04 us (4%)
  between operations  1.67 us (1%)
  loops' own time  1.48 us (1%)
    all_gather x1, blocking collectives, on_device(): key_rows = lax.all_gather(both_keys, 'seq', axis=0, tiled=True)  30.9 us
    all_gather x1, blocking collectives, on_device(): value_rows = lax.all_gather(both_values, 'seq', axis=0, tiled=True)  30.9 us
    all_gather x1, blocking collectives, on_device(): new_keys = lax.all_gather(decode_new_keys, 'seq', axis=0, tiled=True)  18.2 us
    all_gather x1, blocking collectives, on_device(): new_values = lax.all_gather(decode_new_values, 'seq', axis=0, tiled=True)  16.3 us
    ppermute x3, starting transfers between devices, on_device(): from_right = lax.ppermute(from_right, 'seq', left)  10.6 us
    ppermute x4, waiting for transfers between devices, on_device(): from_left = lax.ppermute(from_left, 'seq', forward)  8.48 us
    unnamed x27, local copies, waits for them, and re-layouts  5.89 us
    ppermute x4, starting transfers between devices, on_device(): from_left = lax.ppermute(from_left, 'seq', forward)  4.98 us
  transfers between devices with their start and end apart: 7, of which 3 were waited for; matrix products, arithmetic and copies ran while one was open for 7% of the time, Pallas kernels for 0%

profile of v1, /device:TPU:0, one launch (start us, length us, event | category | flops | bytes accessed | tf_op | source)
XLA Modules:
  0.0 140.6 jit_solution(13253546935683407031)
XLA Ops:
  0.6 0.0 copy-start
  0.7 0.8 copy.86
  1.5 3.0 %collective-permute-start.1 = (bf16[2,32,128]{2,0,1:T(2,128)(2,1)S(1)}, bf16[2,32,128]{2,0,1:T(2,128)(2,1)S(1)}, u32[]{:S(2)}, u32[]{:S(2)}) collective-permute-start(bf16[2,32,128]{2,0,1:T(2,128)(2,1)S(1)} %copy.86), channel_id=1, source_target_pairs={{0,2},{2,4},{4,6},{6,8},{8,10},{10,12},{12,14},{14,0},{1,3},{3,5},... | collective-permute-start | bytes 49160 | tf_op jit(solution)/shard_map/ppermute | solution.py:156
  4.5 3.1 %collective-permute-start = (bf16[2,32,128]{2,0,1:T(2,128)(2,1)S(1)}, bf16[2,32,128]{2,0,1:T(2,128)(2,1)S(1)}, u32[]{:S(2)}, u32[]{:S(2)}) collective-permute-start(bf16[2,32,128]{2,0,1:T(2,128)(2,1)S(1)} %copy.86), channel_id=1, source_target_pairs={{0,14},{2,0},{4,2},{6,4},{8,6},{10,8},{12,10},{14,12},{1,15},{3,1}... | collective-permute-start | bytes 49160 | tf_op jit(solution)/shard_map/ppermute | solution.py:158
  7.6 0.7 iota_compare_fusion.4
  9.0 0.6 copy-done.9
  9.6 0.1 select_reduce_fusion
  9.7 0.1 reduce_sum.68
  9.8 0.7 copy-done.5
  10.5 0.1 pad_maximum_fusion
  10.5 30.9 %all_gather.12 = bf16[640,2,128]{2,1,0:T(2,128)(2,1)S(1)} all-gather(bf16[80,2,128]{2,1,0:T(2,128)(2,1)S(1)} %pad_maximum_fusion), channel_id=1, replica_groups=mesh['groups'=2,'seq'=8,'tp'=2] {'seq'}, dimensions={0}, use_global_device_ids=true | all-gather | bytes 368640 | tf_op jit(solution)/shard_map/all_gather | solution.py:101
  41.5 0.8 copy-done.1
  42.3 0.8 copy-done.4
  43.1 0.1 pad_maximum_fusion.1
  43.1 30.9 %all_gather.13 = bf16[640,2,128]{2,1,0:T(2,128)(2,1)S(1)} all-gather(bf16[80,2,128]{2,1,0:T(2,128)(2,1)S(1)} %pad_maximum_fusion.1), channel_id=1, replica_groups=mesh['groups'=2,'seq'=8,'tp'=2] {'seq'}, dimensions={0}, use_global_device_ids=true | all-gather | bytes 368640 | tf_op jit(solution)/shard_map/all_gather | solution.py:102
  74.2 4.5 %while.14 = (s32[]{:T(128)}, f32[8,2,16]{2,0,1:T(8,128)S(1)}, f32[8,2,16]{2,0,1:T(8,128)S(1)}, f32[8,2,16,128]{3,2,0,1:T(8,128)S(1)}, pred[2,8,288]{2,1,0:T(8,12...) while((s32[]{:T(128)}, f32[8,2,16]{2,0,1:T(8,128)S(1)}, ...), condition=%wide.region_8.9_spmd, body=%wide.region_2.8_spmd.sunk | while | flops 38480640 | bytes 1649647 | solution.py:66
  74.2 0.7 fusion.101
  75.5 0.9 conditional.4
  75.5 0.3 fusion.89
  75.9 0.2 fusion.4
  76.1 0.3 fusion.2
  76.4 0.7 fusion.101
  77.8 0.9 conditional.4
  77.8 0.3 fusion.89
  78.1 0.2 fusion.4
  78.4 0.3 fusion.2
  78.7 0.6 convert_reduce_fusion.1
  79.3 0.2 convert_reduce_fusion
  79.5 0.1 fusion.54
  79.6 0.6 copy-done.11
  80.2 0.1 select_reduce_fusion.1
  80.3 0.1 iota_compare_fusion.3
  80.3 0.6 copy-done.7
  80.9 18.2 %all_gather.14 = bf16[16,2,128]{2,1,0:T(2,128)(2,1)S(1)} all-gather(bf16[2,2,128]{2,1,0:T(2,128)(2,1)S(1)} %copy-done.7), channel_id=1, replica_groups=mesh['groups'=2,'seq'=8,'tp'=2] {'seq'}, dimensions={0}, use_global_device_ids=true | all-gather | bytes 9216 | tf_op jit(solution)/shard_map/all_gather | solution.py:140
  99.2 0.3 fusion.39
  99.4 0.4 copy-done.8
  99.8 16.3 %all_gather.15 = bf16[16,2,128]{2,1,0:T(2,128)(2,1)S(1)} all-gather(bf16[2,2,128]{2,1,0:T(2,128)(2,1)S(1)} %copy-done.8), channel_id=1, replica_groups=mesh['groups'=2,'seq'=8,'tp'=2] {'seq'}, dimensions={0}, use_global_device_ids=true | all-gather | bytes 9216 | tf_op jit(solution)/shard_map/all_gather | solution.py:141
  116.2 0.3 fusion.38
  116.4 0.7 conditional.2
  116.4 0.2 fusion.90
  116.7 0.2 fusion.20
  116.9 0.2 fusion.16
  117.2 0.1 divide_convert_fusion
  117.3 0.6 copy-done.2
  117.9 0.2 fusion.65
  118.1 0.7 iota_compare_fusion.5
  118.9 0.6 copy.85
  119.5 2.0 %collective-permute-start.3 = (bf16[2,32,128]{2,0,1:T(2,128)(2,1)S(1)}, bf16[2,32,128]{2,0,1:T(2,128)(2,1)S(1)}, u32[]{:S(2)}, u32[]{:S(2)}) collective-permute-start(bf16[2,32,128]{2,0,1:T(2,128)(2,1)S(1)} %collective-permute-done.1), channel_id=1, source_target_pairs={{0,2},{2,4},{4,6},{6,8},{8,10},{10,12},{12,14},{14,0},{1,3},{3,5},... | collective-permute-start | bytes 49160 | tf_op jit(solution)/shard_map/ppermute | solution.py:156
  121.5 2.8 %collective-permute-start.2 = (bf16[2,32,128]{2,0,1:T(2,128)(2,1)S(1)}, bf16[2,32,128]{2,0,1:T(2,128)(2,1)S(1)}, u32[]{:S(2)}, u32[]{:S(2)}) collective-permute-start(bf16[2,32,128]{2,0,1:T(2,128)(2,1)S(1)} %collective-permute-done), channel_id=1, source_target_pairs={{0,14},{2,0},{4,2},{6,4},{8,6},{10,8},{12,10},{14,12},{1,15},{3,1}... | collective-permute-start | bytes 49160 | tf_op jit(solution)/shard_map/ppermute | solution.py:158
  124.2 0.2 convolution_add_fusion.4
  124.5 0.2 convolution_add_fusion.3
  124.7 1.3 collective-permute-done.3
  126.0 0.2 fusion.74
  126.2 4.8 %collective-permute-start.4 = (bf16[2,32,128]{2,0,1:T(2,128)(2,1)S(1)}, bf16[2,32,128]{2,0,1:T(2,128)(2,1)S(1)}, u32[]{:S(2)}, u32[]{:S(2)}) collective-permute-start(bf16[2,32,128]{2,0,1:T(2,128)(2,1)S(1)} %collective-permute-done.2), channel_id=1, source_target_pairs={{0,14},{2,0},{4,2},{6,4},{8,6},{10,8},{12,10},{14,12},{1,15},{3,1}... | collective-permute-start | bytes 49160 | tf_op jit(solution)/shard_map/ppermute | solution.py:158
  131.0 0.2 fusion.33
  131.2 1.2 collective-permute-done.5
  132.4 0.2 fusion.79
  132.6 0.2 fusion.32
  132.8 6.0 %collective-permute-done.6 = bf16[2,32,128]{2,0,1:T(2,128)(2,1)S(1)} collective-permute-done((bf16[2,32,128]{2,0,1:T(2,128)(2,1)S(1)}, bf16[2,32,128]{2,0,1:T(2,128)(2,1)S(1)}, u32[]{:S(2)}, u32[]{:S(2)}) %collective-permute-start.6) | collective-permute-done | bytes 16416 | tf_op jit(solution)/shard_map/ppermute | solution.py:156
  138.8 0.2 fusion.37
  139.0 0.1 fusion.48
  139.2 0.3 fusion.91
  139.5 0.2 fusion.42
  139.8 0.9 fusion.36
  (49 shorter events, 0.4 us)
Async XLA Ops:
  0.6 138.6 %copy-start = (bf16[4,256,2,128]{3,2,1,0:T(2,128)(2,1)S(1)}, bf16[4,256,2,128]{3,2,1,0:T(2,128)(2,1)}, u32[]{:S(2)}) copy-start(bf16[4,256,2,128]{3,2,1,0:T(2,128)(2,1)} %param.28) | copy-start | bytes 1572868
  0.6 9.2 %copy-start.3 = (bf16[72,2,128]{2,1,0:T(2,128)(2,1)S(1)}, bf16[72,2,128]{2,1,0:T(2,128)(2,1)}, u32[]{:S(2)}) copy-start(bf16[72,2,128]{2,1,0:T(2,128)(2,1)} %param.22) | copy-start | bytes 110596
  1.5 118.1 %collective-permute-start.1 = (bf16[2,32,128]{2,0,1:T(2,128)(2,1)S(1)}, bf16[2,32,128]{2,0,1:T(2,128)(2,1)S(1)}, u32[]{:S(2)}, u32[]{:S(2)}) collective-permute-start(bf16[2,32,128]{2,0,1:T(2,128)(2,1)S(1)} %copy.86), channel_id=1, source_target_pairs={{0,2},{2,4},{4,6},{6,8},{8,10},{10,12},{12,14},{14,0},{1,3},{3,5},... | collective-permute-start | bytes 49160 | tf_op jit(solution)/shard_map/ppermute | solution.py:156
  4.5 117.0 %collective-permute-start = (bf16[2,32,128]{2,0,1:T(2,128)(2,1)S(1)}, bf16[2,32,128]{2,0,1:T(2,128)(2,1)S(1)}, u32[]{:S(2)}, u32[]{:S(2)}) collective-permute-start(bf16[2,32,128]{2,0,1:T(2,128)(2,1)S(1)} %copy.86), channel_id=1, source_target_pairs={{0,14},{2,0},{4,2},{6,4},{8,6},{10,8},{12,10},{14,12},{1,15},{3,1}... | collective-permute-start | bytes 49160 | tf_op jit(solution)/shard_map/ppermute | solution.py:158
  8.9 0.7 copy-start.9
  9.8 0.7 copy-start.5
  41.5 0.8 copy-start.1
  42.3 0.8 copy-start.4
  42.3 0.8 copy-start.6
  74.2 4.5 %copy-start.10 = (s32[16,1]{0,1:T(1,128)S(1)}, s32[16,1]{0,1:T(1,128)}, u32[]{:S(2)}) copy-start(s32[16,1]{0,1:T(1,128)} %param.30) | copy-start | bytes 196
  79.5 0.7 copy-start.11
  80.3 0.7 copy-start.7
  99.2 0.7 copy-start.8
  117.2 0.7 copy-start.2
  119.5 6.4 %collective-permute-start.3 = (bf16[2,32,128]{2,0,1:T(2,128)(2,1)S(1)}, bf16[2,32,128]{2,0,1:T(2,128)(2,1)S(1)}, u32[]{:S(2)}, u32[]{:S(2)}) collective-permute-start(bf16[2,32,128]{2,0,1:T(2,128)(2,1)S(1)} %collective-permute-done.1), channel_id=1, source_target_pairs={{0,2},{2,4},{4,6},{6,8},{8,10},{10,12},{12,14},{14,0},{1,3},{3,5},... | collective-permute-start | bytes 49160 | tf_op jit(solution)/shard_map/ppermute | solution.py:156
  121.5 4.7 %collective-permute-start.2 = (bf16[2,32,128]{2,0,1:T(2,128)(2,1)S(1)}, bf16[2,32,128]{2,0,1:T(2,128)(2,1)S(1)}, u32[]{:S(2)}, u32[]{:S(2)}) collective-permute-start(bf16[2,32,128]{2,0,1:T(2,128)(2,1)S(1)} %collective-permute-done), channel_id=1, source_target_pairs={{0,14},{2,0},{4,2},{6,4},{8,6},{10,8},{12,10},{14,12},{1,15},{3,1}... | collective-permute-start | bytes 49160 | tf_op jit(solution)/shard_map/ppermute | solution.py:158
  126.0 6.4 %collective-permute-start.5 = (bf16[2,32,128]{2,0,1:T(2,128)(2,1)S(1)}, bf16[2,32,128]{2,0,1:T(2,128)(2,1)S(1)}, u32[]{:S(2)}, u32[]{:S(2)}) collective-permute-start(bf16[2,32,128]{2,0,1:T(2,128)(2,1)S(1)} %collective-permute-done.3), channel_id=1, source_target_pairs={{0,2},{2,4},{4,6},{6,8},{8,10},{10,12},{12,14},{14,0},{1,3},{3,5},... | collective-permute-start | bytes 49160 | tf_op jit(solution)/shard_map/ppermute | solution.py:156
  126.2 6.4 %collective-permute-start.4 = (bf16[2,32,128]{2,0,1:T(2,128)(2,1)S(1)}, bf16[2,32,128]{2,0,1:T(2,128)(2,1)S(1)}, u32[]{:S(2)}, u32[]{:S(2)}) collective-permute-start(bf16[2,32,128]{2,0,1:T(2,128)(2,1)S(1)} %collective-permute-done.2), channel_id=1, source_target_pairs={{0,14},{2,0},{4,2},{6,4},{8,6},{10,8},{12,10},{14,12},{1,15},{3,1}... | collective-permute-start | bytes 49160 | tf_op jit(solution)/shard_map/ppermute | solution.py:158
  132.4 6.4 %collective-permute-start.6 = (bf16[2,32,128]{2,0,1:T(2,128)(2,1)S(1)}, bf16[2,32,128]{2,0,1:T(2,128)(2,1)S(1)}, u32[]{:S(2)}, u32[]{:S(2)}) collective-permute-start(bf16[2,32,128]{2,0,1:T(2,128)(2,1)S(1)} %collective-permute-done.5), channel_id=1, source_target_pairs={{0,2},{2,4},{4,6},{6,8},{8,10},{10,12},{12,14},{14,0},{1,3},{3,5},... | collective-permute-start | bytes 49160 | tf_op jit(solution)/shard_map/ppermute | solution.py:156
  132.8 6.9 %copy-start.12 = (bf16[4,256,2,128]{3,2,1,0:T(2,128)(2,1)S(1)}, bf16[4,256,2,128]{3,2,1,0:T(2,128)(2,1)}, u32[]{:S(2)}) copy-start(bf16[4,256,2,128]{3,2,1,0:T(2,128)(2,1)} %param.29) | copy-start | bytes 1572868
